TPU v7x, 128 devices: a whole 4x4x4 slice. The times are simulated.
128 devices in a mesh: section: 8 (over x, core), tp: 16 (over z, y).
Axes of the slice: x: 4, y: 4, z: 4, core: 2. Of those that a mesh axis runs over, the one named last changes fastest.
Arguments:
- pending_activation: bfloat16 [8, 128, 4096], P('section'), may hold values from -6 to 6
- admissible_microbatches: bfloat16 [4, 128, 4096], P(None, None, 'tp'), may hold values from -6 to 6
- arrival_plan: int32 [4], replicated, may hold values from 0 to 3, each once
- vanished_hop: int32 [1], replicated, may hold values from 1 to 7
- query_key_value_matrices: bfloat16 [8, 4096, 3, 2048], P('section', None, None, 'tp')
- mixing_projection_matrices: bfloat16 [8, 2048, 4096], P('section', 'tp'), may hold values from -0.125 to 0.125
- normalizer_factors: bfloat16 [8, 4096], P('section'), may hold values from 0.25 to 1.75
Outputs:
- activation_later: bfloat16 [8, 128, 4096], P('section')
- standby_input: bfloat16 [8, 128, 4096], P('section', None, 'tp')
Inputs may be any that keep to these rules, and one draw needn't show every extreme that they name: `vanished_hop`: the preempted section is not the first. `arrival_plan`: each micro-batch index once.
All inputs are finite; a program needn't handle non-finite values.
Results may differ from a plain program's by a relative error of at most 0.013.
Values may be sent and summed in bfloat16 or wider, within the bound.
A program may use at most 64 MiB of HBM per device.

v0:
```python
import functools

import jax
import jax.numpy as jnp
from jax import lax
from jax.experimental import pallas as pl
from jax.experimental.pallas import tpu as pltpu
from jax.sharding import PartitionSpec as P

HD = 128
TICKS = 3
NORM_EPS = 1e-05
MESH = pl.DeviceIdType.MESH
PIECES = 2


def relay_kernel(
    sections, nz, ny,
    lost_ref, plan_ref, pend_ref, pool_ref, win_hbm, wout_hbm, gain_ref,
    later_ref, standby_ref,
    win_ref, wout_ref, w_sem, x_buf, y_buf, acc, qkv, ctx, part, own_part, ry_buf, zs_buf, rz_buf, fwd_buf, last_buf, spare_in,
    ag_zs, ag_zr, ag_ys, ag_yr, rs_zs, rs_zr, rs_ys, rs_yr, sh_s, sh_r,
):
    steps = TICKS + 2
    s = lax.axis_index("section")
    me = lax.axis_index("tp")
    z, y = me // ny, me % ny
    nxt, prv = (s + 1) % sections, (s + sections - 1) % sections
    lost = lost_ref[0]
    devices = nz * ny
    rows, width = x_buf.shape[2], x_buf.shape[3]
    cols = wout_ref.shape[0]
    heads = cols // HD

    def partner(at, mask):
        bit = 1
        while bit <= mask:
            if mask & bit:
                at = at + bit - 2 * bit * ((at // bit) % 2)
            bit *= 2
        return at

    def tp_at(dz, dy):
        return partner(z, dz) * ny + partner(y, dy)

    win_copy = pltpu.make_async_copy(win_hbm, win_ref, w_sem.at[0])
    wout_copy = pltpu.make_async_copy(wout_hbm, wout_ref, w_sem.at[1])
    win_copy.start()
    wout_copy.start()
    barrier = pltpu.get_barrier_semaphore()
    for dz in range(1, nz):
        pl.semaphore_signal(barrier, inc=1, device_id={"section": s, "tp": tp_at(dz, 0)}, device_id_type=MESH)
    for dy in range(1, ny):
        pl.semaphore_signal(barrier, inc=1, device_id={"section": s, "tp": tp_at(0, dy)}, device_id_type=MESH)
    pl.semaphore_signal(barrier, inc=1, device_id={"section": nxt, "tp": me}, device_id_type=MESH)
    pl.semaphore_signal(barrier, inc=1, device_id={"section": prv, "tp": me}, device_id_type=MESH)
    pl.semaphore_wait(barrier, nz + ny)

    def copy_to(src, dst, send, recv, section, tp):
        return pltpu.make_async_remote_copy(
            src_ref=src, dst_ref=dst, send_sem=send, recv_sem=recv,
            device_id={"section": section, "tp": tp}, device_id_type=MESH,
        )

    def span(h):
        return pl.ds(h * (rows // PIECES), rows // PIECES)

    def block_copy(n, slot, h, send, recv, tp):
        return copy_to(x_buf.at[n, slot, span(h)], x_buf.at[n, slot, span(h)], send, recv, s, tp)

    def z_copy(n, h, dz, slot):
        return block_copy(n, slot, h, ag_zs.at[h, dz], ag_zr.at[n, h, dz], tp_at(dz, 0))

    def y_copy(n, h, dz, dy, slot):
        return block_copy(n, slot, h, ag_ys.at[h, dz, dy], ag_yr.at[n, h, dz, dy], tp_at(0, dy))

    def ag_start(n):
        for dz in range(1, nz):
            for h in range(PIECES):
                z_copy(n, h, dz, me).start()
        for dy in range(1, ny):
            for h in range(PIECES):
                y_copy(n, h, 0, dy, me).start()

    def ag_forward(n):
        for dz in range(1, nz):
            for h in range(PIECES):
                z_copy(n, h, dz, tp_at(dz, 0)).wait_recv()
                for dy in range(1, ny):
                    y_copy(n, h, dz, dy, tp_at(dz, 0)).start()

    def ag_finish(n):
        for h in range(PIECES):
            for dz in range(nz):
                for dy in range(1, ny):
                    y_copy(n, h, dz, dy, tp_at(dz, dy)).wait_recv()
            for dz in range(1, nz):
                z_copy(n, h, dz, me).wait_send()
            for dz in range(nz):
                for dy in range(1, ny):
                    y_copy(n, h, dz, dy, tp_at(dz, 0)).wait_send()

    def layer(n):
        def add_sum(j, total):
            return total + jnp.sum(x_buf[n, j].astype(jnp.float32), axis=-1, keepdims=True)

        count = float(devices * width)
        mean = lax.fori_loop(0, devices, add_sum, jnp.zeros((rows, 1), jnp.float32)) / count

        def add_square(j, total):
            centered = x_buf[n, j].astype(jnp.float32) - mean
            return total + jnp.sum(centered * centered, axis=-1, keepdims=True)

        var = lax.fori_loop(0, devices, add_square, jnp.zeros((rows, 1), jnp.float32)) / count
        rstd = lax.rsqrt(var + NORM_EPS)

        @pl.when(n == 0)
        def _():
            win_copy.wait()
            wout_copy.wait()

        acc[...] = jnp.zeros_like(acc)

        def project(j, carry):
            at = pl.ds(pl.multiple_of(j * width, 128), width)
            gain = gain_ref[:, at].astype(jnp.float32)
            normed = ((x_buf[n, j].astype(jnp.float32) - mean) * rstd * gain).astype(jnp.bfloat16)
            for i in range(3):
                acc[:, i * cols:(i + 1) * cols] += jnp.dot(
                    normed, win_ref[i, at, :], preferred_element_type=jnp.float32
                )
            return carry

        lax.fori_loop(0, devices, project, 0)
        qkv[...] = acc[...].astype(jnp.bfloat16)
        causal = lax.broadcasted_iota(jnp.int32, (rows, rows), 0) >= lax.broadcasted_iota(jnp.int32, (rows, rows), 1)
        for h in range(heads):
            q = qkv[:, h * HD:(h + 1) * HD]
            k = qkv[:, cols + h * HD:cols + (h + 1) * HD]
            v = qkv[:, 2 * cols + h * HD:2 * cols + (h + 1) * HD]
            scores = lax.dot_general(q, k, (((1,), (1,)), ((), ())), preferred_element_type=jnp.float32)
            scores = jnp.where(causal, scores * HD ** (-0.5), -jnp.inf)
            weights = jnp.exp(scores - jnp.max(scores, axis=-1, keepdims=True))
            probs = (weights / jnp.sum(weights, axis=-1, keepdims=True)).astype(jnp.bfloat16)
            ctx[:, h * HD:(h + 1) * HD] = jnp.dot(probs, v, preferred_element_type=jnp.float32).astype(jnp.bfloat16)

        def partial_for(tp):
            at = pl.ds(pl.multiple_of(tp * width, 128), width)
            return jnp.dot(ctx[...], wout_ref[:, at], preferred_element_type=jnp.float32)

        order = list(range(nz - 1, -1, -1))
        sends, got = [], {}
        for dz in order:
            for dy in range(1, ny):
                part[dy - 1, dz] = partial_for(tp_at(dz, dy)).astype(jnp.bfloat16)
                for h in range(PIECES):
                    got[dz, dy, h] = copy_to(part.at[dy - 1, dz, span(h)], ry_buf.at[n, dy - 1, dz, span(h)],
                                             rs_ys.at[h, dz, dy], rs_yr.at[n, h, dz, dy], s, tp_at(0, dy))
                    got[dz, dy, h].start()
        for dz in order:
            own_part[dz] = partial_for(tp_at(dz, 0))
        for dz in order:
            for h in range(PIECES):
                total = own_part[dz, span(h)]
                for dy in range(1, ny):
                    got[dz, dy, h].wait_recv()
                    total = total + ry_buf[n, dy - 1, dz, span(h)].astype(jnp.float32)
                if dz:
                    zs_buf[dz - 1, span(h)] = total.astype(jnp.bfloat16)
                    sends.append(copy_to(zs_buf.at[dz - 1, span(h)], rz_buf.at[n, dz - 1, span(h)],
                                         rs_zs.at[h, dz], rs_zr.at[n, h, dz], s, tp_at(dz, 0)))
                    sends[-1].start()
                else:
                    own_part[0, span(h)] = total

        @pl.when((s == 0) & (n < TICKS - 1))
        def _():
            ag_forward(n + 1)

        @pl.when(n == TICKS + 1)
        def _():
            ag_forward(steps)

        total = own_part[0]
        for copy in sends:
            copy.wait_recv()
        for dz in range(1, nz):
            total = total + rz_buf[n, dz - 1].astype(jnp.float32)
        y_buf[n] = (x_buf[n, me].astype(jnp.float32) + total).astype(jnp.bfloat16)
        for copy in list(got.values()) + sends:
            copy.wait_send()

    def needed(section, n):
        tail = (n <= TICKS) | (section > 2) | (section == 0)
        live = (section + TICKS - 1 >= n) | ((section == 0) & (n == TICKS + 1))
        if sections <= TICKS + 1:
            live = live & ((section != sections - 1) | (n != TICKS - 1))
        return live & tail

    def passes(section, n):
        return needed(section, n) & (n > 0) & ((section > 0) | (n == TICKS + 1))

    def shift_copy(n):
        return copy_to(fwd_buf, x_buf.at[n, me], sh_s.at[0], sh_r.at[n], nxt, me)

    def pick(cond, a, b):
        return jnp.where(jnp.full(a.shape, cond), a, b)

    def own_rows():
        settled = pick((s < lost) | (s - TICKS + 1 > lost), y_buf[TICKS - 1], y_buf[TICKS])
        return pick(s == lost, y_buf[0], settled)

    out_copy = copy_to(last_buf.at[0], x_buf.at[steps, me], sh_s.at[1], sh_r.at[steps], nxt, me)

    def step(n, carry):
        @pl.when(needed(s, n))
        def _():
            @pl.when(n == 0)
            def _():
                for j in range(devices):
                    rows_j = pend_ref[0, :, j * width:(j + 1) * width]
                    x_buf[0, j] = pick(s == lost, jnp.zeros_like(rows_j), rows_j)

            @pl.when(passes(s, n))
            def _():
                shift_copy(n).wait_recv()
                ag_start(n)
                ag_forward(n)

            @pl.when(n > 0)
            def _():
                ag_finish(n)

            @pl.when((s == 0) & (n < TICKS - 1))
            def _():
                x_buf[n + 1, me] = pool_ref[plan_ref[n]]
                ag_start(n + 1)

            @pl.when(n == TICKS + 1)
            def _():
                out_copy.wait_recv()
                ag_start(steps)

            layer(n)

        @pl.when(jnp.logical_not(needed(s, n)))
        def _():
            y_buf[n] = jnp.zeros((rows, width), jnp.bfloat16)

            @pl.when(n == TICKS + 1)
            def _():
                out_copy.wait_recv()
                ag_start(steps)
                ag_forward(steps)

        @pl.when((n < steps - 1) & passes(nxt, n + 1))
        def _():
            fwd_buf[...] = y_buf[n]

            @pl.when((n == TICKS) & (s == sections - 1))
            def _():
                fwd_buf[...] = own_rows()

            copy = shift_copy(n + 1)
            copy.start()
            copy.wait_send()

        @pl.when(n == TICKS)
        def _():
            final = pick(s == lost, y_buf[TICKS], own_rows())
            final = pick(nxt == 0, pool_ref[plan_ref[TICKS - 1]], final)
            last_buf[0] = pick(nxt == lost, jnp.zeros_like(final), final)
            out_copy.start()

        return carry

    lax.fori_loop(0, steps, step, 0)

    settled = pick((s - 1 < lost) | (s - TICKS > lost), y_buf[TICKS], y_buf[TICKS + 1])
    spare = pick(s - 1 == lost, y_buf[1], settled)
    spare = pick(s == 0, y_buf[TICKS + 1], spare)
    last_buf[1] = spare
    spare_copy = copy_to(last_buf.at[1], spare_in, sh_s.at[0], sh_r.at[0], nxt, me)
    spare_copy.start()
    ag_finish(steps)
    for j in range(devices):
        later_ref[0, :, j * width:(j + 1) * width] = x_buf[steps, j]
    spare_copy.wait_recv()
    standby_ref[0] = spare_in[...]
    out_copy.wait_send()
    spare_copy.wait_send()


def solution(mesh):
    sections, devices = mesh.shape["section"], mesh.shape["tp"]
    ny = 1
    while (2 * ny) * (2 * ny) <= devices and devices % (2 * ny) == 0:
        ny *= 2
    nz = devices // ny

    def per_device(pend, pool, plan, lost, win, wout, gain):
        rows, hidden = pend.shape[1], pend.shape[2]
        width = hidden // devices
        cols = win.shape[3]
        slots = TICKS + 3
        win = jnp.transpose(win[0], (1, 0, 2))
        vmem = pl.BlockSpec(memory_space=pltpu.VMEM)
        smem = pl.BlockSpec(memory_space=pltpu.SMEM)
        hbm = pl.BlockSpec(memory_space=pl.ANY)
        bf = functools.partial(pltpu.VMEM, dtype=jnp.bfloat16)
        dma = pltpu.SemaphoreType.DMA
        return pl.pallas_call(
            functools.partial(relay_kernel, sections, nz, ny),
            out_shape=(
                jax.ShapeDtypeStruct((1, rows, hidden), jnp.bfloat16),
                jax.ShapeDtypeStruct((1, rows, width), jnp.bfloat16),
            ),
            in_specs=[smem, smem, vmem, vmem, hbm, hbm, vmem],
            out_specs=(vmem, vmem),
            scratch_shapes=[
                bf((3, hidden, cols)),
                bf((cols, hidden)),
                dma((2,)),
                bf((slots, devices, rows, width)),
                bf((slots, rows, width)),
                pltpu.VMEM((rows, 3 * cols), jnp.float32),
                bf((rows, 3 * cols)),
                bf((rows, cols)),
                bf((ny - 1, nz, rows, width)),
                pltpu.VMEM((nz, rows, width), jnp.float32),
                bf((slots, ny - 1, nz, rows, width)),
                bf((nz - 1, rows, width)),
                bf((slots, nz - 1, rows, width)),
                bf((rows, width)),
                bf((2, rows, width)),
                bf((rows, width)),
                dma((PIECES, nz)), dma((slots, PIECES, nz)), dma((PIECES, nz, ny)), dma((slots, PIECES, nz, ny)),
                dma((PIECES, nz)), dma((slots, PIECES, nz)), dma((PIECES, nz, ny)), dma((slots, PIECES, nz, ny)),
                dma((2,)), dma((slots,)),
            ],
            compiler_params=pltpu.CompilerParams(
                collective_id=0, has_side_effects=True, vmem_limit_bytes=60 * 1024 * 1024
            ),
        )(lost, plan, pend, pool, win, wout[0], gain)

    placed = (
        P("section", None, None),
        P(None, None, "tp"),
        P(),
        P(),
        P("section", None, None, "tp"),
        P("section", "tp", None),
        P("section", None),
    )
    return jax.shard_map(
        per_device,
        mesh=mesh,
        in_specs=placed,
        out_specs=(P("section", None, None), P("section", None, "tp")),
        check_vma=False,
    )
```

profile of v0, /device:TPU:4, one launch (start us, length us, event | category | flops | bytes accessed | tf_op | source)
XLA Modules:
  0.0 196.2 jit_solution(7498445208741757904)
XLA Ops:
  1.3 191.1 %shard_map.86 = (bf16[1,128,4096]{2,1,0:T(8,128)(2,1)}, bf16[1,128,256]{2,1,0:T(8,128)(2,1)}) custom-call(s32[1]{0:T(128)S(6)} %copy.11.lost_ref, s32[4]{0:T(128)} %plan_ref.1, bf16[1,128,4096]{2,1,0:T(8,128)(2,1)} %pend_ref.1, bf16[4,128,256]{2,1,0:T(8,128)(2,1)} %pool_ref.1, bf16[3,4096,128]{2,1,0:T(8,128)(2,1)} %bitcast.4, bf16[128,4096]{1,0:T(8,128)(2,1)} %bitcast.5, ...), custom_call_target="tpu_custom_call" | custom-call | tf_op jit(solution)/shard_map/pallas_call | solution.py:312
  192.4 2.3 %copy.12 = bf16[1,128,4096]{2,1,0:T(8,128)(2,1)} copy(bf16[1,128,4096]{2,1,0:T(8,128)(2,1)} %get-tuple-element.4) | data formatting | bytes 2097152
  194.7 1.5 copy.13
where the time goes:
time: 196 us
  Pallas kernels  191 us (97%)
  local copies, waits for them, and re-layouts  3.76 us (2%)
    pallas_call x1, Pallas kernels, per_device(): pl.pallas_call(functools.partial(relay_kernel, sections, nz, ny), out_sha...  191 us

commit v1 on v0

v1 whole, which is shorter than its diff:
```python
import functools

import jax
import jax.numpy as jnp
from jax import lax
from jax.experimental import pallas as pl
from jax.experimental.pallas import tpu as pltpu
from jax.sharding import PartitionSpec as P

HD = 128
TICKS = 3
NORM_EPS = 1e-05
MESH = pl.DeviceIdType.MESH
WAVES = TICKS + 2
CHUNKS = 1
NEAR_FIRST = (1, 3, 2)


def relay_kernel(
    sections, nz, ny,
    lost_ref, plan_ref, pend_hbm, pool_hbm, win_hbm, wout_hbm, gain_ref,
    later_hbm, standby_ref,
    win_ref, colsum_ref, wout_ref, x_buf, b_buf, pool_ref, res_src, res_in, acc, s1, s2, qkv, ctx_own, ctx_in, stage,
    local_sem, ws, wr, xs, xr, c1s, c2s, cr, rs, rr,
):
    s = lax.axis_index("section")
    me = lax.axis_index("tp")
    z, y = me // ny, me % ny
    nxt, prv = (s + 1) % sections, (s + sections - 1) % sections
    devices = nz * ny
    total_rows, width = x_buf.shape[2], x_buf.shape[3]
    rows = total_rows // CHUNKS
    part = rows // 2
    cols = win_ref.shape[1] // 3
    group = ny * width
    lost = lost_ref[0]

    def at(dz, dy):
        return ((z + dz) % nz) * ny + (y + dy) % ny

    def row_of(dz):
        return (z + dz) % nz

    def copy_to(src, dst, send, recv, section, tp):
        return pltpu.make_async_remote_copy(
            src_ref=src, dst_ref=dst, send_sem=send, recv_sem=recv,
            device_id={"section": section, "tp": tp}, device_id_type=MESH,
        )

    def local(src, dst, i):
        return pltpu.make_async_copy(src, dst, local_sem.at[i])

    def pick(cond, a, b):
        return jnp.where(jnp.full(a.shape, cond), a, b)

    def runs(section, n):
        idle = (section == 0) & (n == TICKS)
        idle = idle | (((section == 1) | (section == 2)) & (n == TICKS + 1))
        return jnp.logical_not(idle)

    def gathers(section, n):
        return (n > 0) & jnp.logical_not((section == 1) & (n == TICKS + 1))

    for i in range(3):
        local(win_hbm.at[i], win_ref.at[:, pl.ds(i * cols, cols)], 0).start()
    for j in range(devices):
        local(pend_hbm.at[0, :, pl.ds(j * width, width)], x_buf.at[0, j], 1).start()
    local(pool_hbm, pool_ref, 2).start()

    barrier = pltpu.get_barrier_semaphore()
    for j in range(devices):
        pl.semaphore_signal(barrier, inc=1, device_id={"section": prv, "tp": j}, device_id_type=MESH)
    for k in range(1, nz):
        pl.semaphore_signal(barrier, inc=1, device_id={"section": s, "tp": at(k, 0)}, device_id_type=MESH)
    for k in range(1, ny):
        pl.semaphore_signal(barrier, inc=1, device_id={"section": s, "tp": at(0, k)}, device_id_type=MESH)
    pl.semaphore_wait(barrier, devices + nz + ny - 2)

    for dz in (0,) + NEAR_FIRST:
        for dy in (0,) + NEAR_FIRST:
            t = at(dz, dy)
            copy_to(wout_hbm.at[:, pl.ds(pl.multiple_of(t * width, 128), width)],
                    wout_ref.at[pl.ds(pl.multiple_of(me * cols, 128), cols)], ws, wr, nxt, t).start()

    pltpu.make_async_copy(win_ref, win_ref, local_sem.at[0]).wait()
    eye = lax.broadcasted_iota(jnp.int32, (width, width), 0) == lax.broadcasted_iota(jnp.int32, (width, width), 1)
    colsum_ref[...] = jnp.zeros_like(colsum_ref)

    def fold(j, carry):
        span = pl.ds(pl.multiple_of(j * width, width), width)
        scale = jnp.where(eye, jnp.broadcast_to(gain_ref[:, span].astype(jnp.float32), (width, width)), 0.0)
        scaled = jnp.dot(scale.astype(jnp.bfloat16), win_ref[span, :], preferred_element_type=jnp.float32)
        scaled = scaled.astype(jnp.bfloat16)
        win_ref[span, :] = scaled
        colsum_ref[...] += jnp.sum(scaled.astype(jnp.float32).reshape(width // 8, 8, 3 * cols), axis=0)
        return carry

    lax.fori_loop(0, devices, fold, 0)
    colsum_ref[...] = jnp.broadcast_to(jnp.sum(colsum_ref[...], axis=0, keepdims=True), colsum_ref.shape)
    pltpu.make_async_copy(x_buf.at[0], x_buf.at[0], local_sem.at[1]).wait()
    pltpu.make_async_copy(pool_ref, pool_ref, local_sem.at[2]).wait()
    own = x_buf[0, me]
    res_src[...] = pick(s == lost, jnp.zeros_like(own), own)

    def span_of(c):
        return pl.ds(c * rows, rows)

    def half_of(c, h):
        return pl.ds(c * rows + h * part, part)

    def residual(n, c, src):
        return copy_to(src, res_in.at[n, span_of(c)], rs.at[n, c], rr.at[n, c], nxt, me)

    for c in range(CHUNKS):
        residual(0, c, res_src.at[span_of(c)]).start()

    def x_copy(n, c, h, slot, tp):
        ref = x_buf.at[n, slot, half_of(c, h)]
        return copy_to(ref, ref, xs.at[n], xr.at[n, c, h, slot], s, tp)

    def x_send(n, c):
        for k in NEAR_FIRST:
            x_copy(n, c, 0, me, at(k, 0)).start()
            x_copy(n, c, 1, me, at(0, k)).start()
        for k in NEAR_FIRST:
            x_copy(n, c, 1, me, at(k, 0)).start()
            x_copy(n, c, 0, me, at(0, k)).start()

    def forward(copy, n, c, first):
        for k in first:
            copy(n, c, 0, at(k, 0), me).wait_recv()
            for m in NEAR_FIRST:
                copy(n, c, 0, at(k, 0), at(0, m)).start()
            copy(n, c, 1, at(0, k), me).wait_recv()
            for m in NEAR_FIRST:
                copy(n, c, 1, at(0, k), at(m, 0)).start()

    def settle(copy, n, c, dz):
        for k in (0,) + NEAR_FIRST:
            if k:
                copy(n, c, 0, at(dz, k), me).wait_recv()
            if dz:
                copy(n, c, 1, at(dz, k), me).wait_recv()

    def c_copy(n, c, h, slot, tp):
        ref = ctx_in.at[n, slot, half_of(c, h)]
        return copy_to(ref, ref, c2s.at[n], cr.at[n, c, h, slot], s, tp)

    def c_send(n, c):
        for k in (0,) + NEAR_FIRST:
            for h, tp in ((0, at(k, 0)), (1, at(0, k))):
                copy_to(ctx_own.at[n, half_of(c, h)], ctx_in.at[n, me, half_of(c, h)],
                        c1s.at[n], cr.at[n, c, h, me], nxt, tp).start()

    def layer(n, c):
        dead = (s == lost) & (n == 0)
        span = span_of(c)
        own = x_buf[n, me, span]
        own = pick(dead, jnp.zeros_like(own), own).astype(jnp.float32)
        shift = jnp.broadcast_to(jnp.sum(own, axis=-1, keepdims=True) / width, (rows, width))
        for i, dz in enumerate((0,) + NEAR_FIRST):
            @pl.when(n > 0)
            def _():
                settle(x_copy, n, c, dz)

            zr = row_of(dz)
            blocks, sums, squares = [], None, None
            for k in range(ny):
                block = x_buf[n, zr * ny + k, span]
                block = pick(dead, jnp.zeros_like(block), block)
                blocks.append(block)
                moved = block.astype(jnp.float32) - shift
                square = moved * moved
                sums = moved if sums is None else sums + moved
                squares = square if squares is None else squares + square
            wide = jnp.concatenate(blocks, axis=1)
            weights = win_ref[pl.ds(pl.multiple_of(zr * group, group), group), :]
            product = jnp.dot(wide, weights, preferred_element_type=jnp.float32)
            sums = sums[:, :width // 2] + sums[:, width // 2:]
            squares = squares[:, :width // 2] + squares[:, width // 2:]
            if i == 0:
                acc[...] = product
                s1[...] = sums
                s2[...] = squares
            elif i < nz - 1:
                acc[...] += product
                s1[...] += sums
                s2[...] += squares
            else:
                product = acc[...] + product
                sums = s1[...] + sums
                squares = s2[...] + squares
        count = float(devices * width)
        off = jnp.sum(sums, axis=-1, keepdims=True) / count
        var = jnp.sum(squares, axis=-1, keepdims=True) / count - off * off
        rstd = lax.rsqrt(var + NORM_EPS)
        mean = shift[:, :1] + off
        qkv[span] = ((product - mean * colsum_ref[:1]) * rstd).astype(jnp.bfloat16)
        seen = (c + 1) * rows
        q = qkv[span, :HD]
        k = qkv[:seen, HD:2 * HD]
        v = qkv[:seen, 2 * HD:]
        scores = lax.dot_general(q, k, (((1,), (1,)), ((), ())), preferred_element_type=jnp.float32)
        query = lax.broadcasted_iota(jnp.int32, (rows, seen), 0) + c * rows
        causal = query >= lax.broadcasted_iota(jnp.int32, (rows, seen), 1)
        scores = jnp.where(causal, scores * HD ** (-0.5), -jnp.inf)
        weights = jnp.exp(scores - jnp.max(scores, axis=-1, keepdims=True))
        probs = (weights / jnp.sum(weights, axis=-1, keepdims=True)).astype(jnp.bfloat16)
        ctx_own[n, span] = jnp.dot(probs, v, preferred_element_type=jnp.float32).astype(jnp.bfloat16)
        c_send(n, c)

    def finish(n, c):
        if c == 0:
            @pl.when(n == 0)
            def _():
                pltpu.make_async_copy(wout_ref, wout_ref, wr).wait()

        span = span_of(c)
        residual(n, c, res_src.at[span]).wait_recv()
        total = res_in[n, span].astype(jnp.float32)
        for dz in (0,) + NEAR_FIRST:
            settle(c_copy, n, c, dz)
            zr = row_of(dz)
            wide = jnp.concatenate([ctx_in[n, zr * ny + k, span] for k in range(ny)], axis=1)
            weights = wout_ref[pl.ds(pl.multiple_of(zr * ny * cols, ny * cols), ny * cols), :]
            total = total + jnp.dot(wide, weights, preferred_element_type=jnp.float32)
        b_buf[n + 1, span] = total.astype(jnp.bfloat16)

    def advance(n, c):
        span = span_of(c)

        @pl.when(s == 0)
        def _():
            settled = pick(sections - TICKS > lost, b_buf[TICKS, span], b_buf[TICKS + 1, span])
            settled = pick(sections - 1 == lost, b_buf[1, span], settled)
            x_buf[n + 1, me, span] = pick(n < TICKS, pool_ref[plan_ref[n], span], settled)

        @pl.when(s != 0)
        def _():
            x_buf[n + 1, me, span] = b_buf[n + 1, span]

        @pl.when(gathers(s, n + 1))
        def _():
            x_send(n + 1, c)

        @pl.when(runs(s, n + 1))
        def _():
            residual(n + 1, c, x_buf.at[n + 1, me, span]).start()

    def output():
        early = (s == 0) | (s < lost) | (s - TICKS > lost)
        for j in range(devices):
            block = pick(early, x_buf[TICKS, j], x_buf[TICKS + 1, j])
            stage[j] = pick(s == lost, jnp.zeros_like(block), block)
        for j in range(devices):
            local(stage.at[j], later_hbm.at[0, :, pl.ds(j * width, width)], 3).start()

    def step(n, carry):
        for c in range(CHUNKS):
            @pl.when(gathers(s, n))
            def _():
                forward(x_copy, n, c, NEAR_FIRST)

            if c:
                @pl.when(runs(prv, n))
                def _():
                    forward(c_copy, n, c - 1, (0,) + NEAR_FIRST)

            @pl.when(runs(s, n))
            def _():
                layer(n, c)

            @pl.when(gathers(s, n) & jnp.logical_not(runs(s, n)))
            def _():
                for dz in (0,) + NEAR_FIRST:
                    settle(x_copy, n, c, dz)

        @pl.when(n == WAVES - 1)
        def _():
            output()

        for c in range(CHUNKS):
            @pl.when(runs(prv, n))
            def _():
                if c == CHUNKS - 1:
                    forward(c_copy, n, c, (0,) + NEAR_FIRST)
                finish(n, c)

            @pl.when(jnp.logical_not(runs(prv, n)))
            def _():
                b_buf[n + 1, span_of(c)] = jnp.zeros((rows, width), jnp.bfloat16)

            @pl.when(n < WAVES - 1)
            def _():
                advance(n, c)

        return carry

    lax.fori_loop(0, WAVES, step, 0)

    settled = pick((s - 2 < lost) | (s - 2 - TICKS + 1 > lost), b_buf[TICKS + 1], b_buf[TICKS + 2])
    settled = pick((s + sections - 2) % sections == lost, b_buf[2], settled)
    last = sections - 2
    wrapped = pick((last < lost) | (last - TICKS + 1 > lost), b_buf[TICKS + 1], b_buf[TICKS + 2])
    wrapped = pick(last == lost, b_buf[2], wrapped)
    settled = pick(s == 0, wrapped, settled)
    standby_ref[0] = pick(s == 1, b_buf[TICKS + 2], settled)

    pltpu.make_async_copy(wout_ref, wout_ref, ws).wait()
    pltpu.make_async_copy(stage, stage, local_sem.at[3]).wait()

    def drain(n, carry):
        @pl.when(gathers(s, n))
        def _():
            ref = x_buf.at[0, pl.ds(0, devices - 1)]
            pltpu.make_async_copy(ref, ref, xs.at[n]).wait()

        @pl.when(runs(s, n))
        def _():
            ref = ctx_in.at[0, pl.ds(0, (nz + ny) // 2)]
            pltpu.make_async_copy(ref, ref, c1s.at[n]).wait()
            for c in range(CHUNKS):
                residual(n, c, res_src.at[span_of(c)]).wait_send()

        @pl.when(runs(prv, n))
        def _():
            ref = ctx_in.at[0, pl.ds(0, devices - (nz + ny) // 2)]
            pltpu.make_async_copy(ref, ref, c2s.at[n]).wait()

        return carry

    lax.fori_loop(0, WAVES, drain, 0)


def solution(mesh):
    sections, devices = mesh.shape["section"], mesh.shape["tp"]
    ny = 1
    while (2 * ny) * (2 * ny) <= devices and devices % (2 * ny) == 0:
        ny *= 2
    nz = devices // ny

    def per_device(pend, pool, plan, lost, win, wout, gain):
        rows, hidden = pend.shape[1], pend.shape[2]
        width = hidden // devices
        cols = win.shape[3]
        win = jnp.transpose(win[0], (1, 0, 2))
        vmem = pl.BlockSpec(memory_space=pltpu.VMEM)
        smem = pl.BlockSpec(memory_space=pltpu.SMEM)
        hbm = pl.BlockSpec(memory_space=pl.ANY)
        bf = functools.partial(pltpu.VMEM, dtype=jnp.bfloat16)
        f32 = functools.partial(pltpu.VMEM, dtype=jnp.float32)
        dma = pltpu.SemaphoreType.DMA
        chunk = rows // CHUNKS
        return pl.pallas_call(
            functools.partial(relay_kernel, sections, nz, ny),
            out_shape=(
                jax.ShapeDtypeStruct((1, rows, hidden), jnp.bfloat16),
                jax.ShapeDtypeStruct((1, rows, width), jnp.bfloat16),
            ),
            in_specs=[smem, smem, hbm, hbm, hbm, hbm, vmem],
            out_specs=(hbm, vmem),
            scratch_shapes=[
                bf((hidden, 3 * cols)),
                f32((8, 3 * cols)),
                bf((devices * cols, width)),
                bf((WAVES, devices, rows, width)),
                bf((WAVES + 1, rows, width)),
                bf(pool.shape),
                bf((rows, width)),
                bf((WAVES, rows, width)),
                f32((chunk, 3 * cols)),
                f32((chunk, width // 2)),
                f32((chunk, width // 2)),
                bf((rows, 3 * cols)),
                bf((WAVES, rows, cols)),
                bf((WAVES, devices, rows, cols)),
                bf((devices, rows, width)),
                dma((4,)), dma, dma,
                dma((WAVES,)), dma((WAVES, CHUNKS, 2, devices)),
                dma((WAVES,)), dma((WAVES,)), dma((WAVES, CHUNKS, 2, devices)),
                dma((WAVES, CHUNKS)), dma((WAVES, CHUNKS)),
            ],
            compiler_params=pltpu.CompilerParams(
                collective_id=0, has_side_effects=True, vmem_limit_bytes=60 * 1024 * 1024
            ),
        )(lost, plan, pend, pool, win, wout[0], gain)

    placed = (
        P("section", None, None),
        P(None, None, "tp"),
        P(),
        P(),
        P("section", None, None, "tp"),
        P("section", "tp", None),
        P("section", None),
    )
    return jax.shard_map(
        per_device,
        mesh=mesh,
        in_specs=placed,
        out_specs=(P("section", None, None), P("section", None, "tp")),
        check_vma=False,
    )
```

time: 196 us -> 115 us (0.59)
  the two profiles are of different devices: /device:TPU:4 before, /device:TPU:1 now
where the time goes in v1:
time: 115 us; the launch traced here: 114 us
  Pallas kernels  109 us (95%)
  local copies, waits for them, and re-layouts  3.76 us (3%)
  between operations  1.29 us (1%)
    pallas_call x1, Pallas kernels, per_device(): pl.pallas_call(functools.partial(relay_kernel, sections, nz, ny), out_sha...  109 us
    unnamed x2, local copies, waits for them, and re-layouts  3.76 us

profile of v1, /device:TPU:1, one launch (start us, length us, event | category | flops | bytes accessed | tf_op | source)
XLA Modules:
  0.0 113.6 jit_solution(7103074291136159832)
XLA Ops:
  1.3 108.5 %shard_map.86 = (bf16[1,128,4096]{2,1,0:T(8,128)(2,1)}, bf16[1,128,256]{2,1,0:T(8,128)(2,1)}) custom-call(s32[1]{0:T(128)S(6)} %copy.11.lost_ref, s32[4]{0:T(128)} %plan_ref.1, bf16[1,128,4096]{2,1,0:T(8,128)(2,1)} %pend_hbm.1, bf16[4,128,256]{2,1,0:T(8,128)(2,1)} %pool_hbm.1, bf16[3,4096,128]{2,1,0:T(8,128)(2,1)} %bitcast.4, bf16[128,4096]{1,0:T(8,128)(2,1)} %bitcast.5, ...), custom_call_target="tpu_custom_call" | custom-call | tf_op jit(solution)/shard_map/pallas_call | solution.py:354
  109.8 2.3 %copy.12 = bf16[1,128,4096]{2,1,0:T(8,128)(2,1)} copy(bf16[1,128,4096]{2,1,0:T(8,128)(2,1)} %get-tuple-element.4) | data formatting | bytes 2097152
  112.1 1.5 %copy.13 = bf16[1,128,256]{2,1,0:T(8,128)(2,1)} copy(bf16[1,128,256]{2,1,0:T(8,128)(2,1)} %get-tuple-element.5) | data formatting | bytes 131072

commit v2 on v1

--- a/solution.py
+++ b/solution.py
@@ -12,7 +12,7 @@
 NORM_EPS = 1e-05
 MESH = pl.DeviceIdType.MESH
 WAVES = TICKS + 2
-CHUNKS = 1
+CHUNKS = 2
 NEAR_FIRST = (1, 3, 2)
 
 

time: 115 us -> 128 us (1.11)
  Pallas kernels: 109 us -> 122 us
    pallas_call x1, Pallas kernels: 109 us -> 122 us  [per_device(): pl.pallas_call(functools.partial(relay_kernel, sections, nz, ny), out_sha...]
where the time goes in v2:
time: 128 us; the launch traced here: 127 us
  Pallas kernels  122 us (95%)
  local copies, waits for them, and re-layouts  3.76 us (3%)
  between operations  1.29 us (1%)
    pallas_call x1, Pallas kernels, per_device(): pl.pallas_call(functools.partial(relay_kernel, sections, nz, ny), out_sha...  122 us
    unnamed x2, local copies, waits for them, and re-layouts  3.76 us

profile of v2, /device:TPU:1, one launch (start us, length us, event | category | flops | bytes accessed | tf_op | source)
XLA Modules:
  0.0 127.0 jit_solution(2465875924538512131)
XLA Ops:
  1.3 121.9 %shard_map.86 = (bf16[1,128,4096]{2,1,0:T(8,128)(2,1)}, bf16[1,128,256]{2,1,0:T(8,128)(2,1)}) custom-call(s32[1]{0:T(128)S(6)} %copy.11.lost_ref, s32[4]{0:T(128)} %plan_ref.1, bf16[1,128,4096]{2,1,0:T(8,128)(2,1)} %pend_hbm.1, bf16[4,128,256]{2,1,0:T(8,128)(2,1)} %pool_hbm.1, bf16[3,4096,128]{2,1,0:T(8,128)(2,1)} %bitcast.4, bf16[128,4096]{1,0:T(8,128)(2,1)} %bitcast.5, ...), custom_call_target="tpu_custom_call" | custom-call | tf_op jit(solution)/shard_map/pallas_call | solution.py:354
  123.2 2.3 %copy.12 = bf16[1,128,4096]{2,1,0:T(8,128)(2,1)} copy(bf16[1,128,4096]{2,1,0:T(8,128)(2,1)} %get-tuple-element.4) | data formatting | bytes 2097152
  125.5 1.5 %copy.13 = bf16[1,128,256]{2,1,0:T(8,128)(2,1)} copy(bf16[1,128,256]{2,1,0:T(8,128)(2,1)} %get-tuple-element.5) | data formatting | bytes 131072

commit v3 on v2

v3 whole, which is shorter than its diff:
```python
import functools

import jax
import jax.numpy as jnp
from jax import lax
from jax.experimental import pallas as pl
from jax.experimental.pallas import tpu as pltpu
from jax.sharding import PartitionSpec as P

HD = 128
TICKS = 3
NORM_EPS = 1e-05
MESH = pl.DeviceIdType.MESH
WAVES = TICKS + 2
NEAR_FIRST = (1, 3, 2)
PEERS = tuple((k, 0) for k in NEAR_FIRST) + tuple((0, k) for k in NEAR_FIRST)


def relay_kernel(
    sections, nz, ny,
    lost_ref, plan_ref, pend_hbm, pool_hbm, win_hbm, wout_hbm, gain_hbm,
    later_hbm, standby_ref,
    win_ref, gain_ref, colsum_ref, wsrc_ref, wout_ref, x_buf, b_buf, pool_ref, res_src, res_in, acc, s1, s2, own_sum, ctx_in, sums_out, sums_in, stage,
    local_sem, ws, wr, xs, xr, cs, cr, ps, pr, rs, rr,
):
    s = lax.axis_index("section")
    me = lax.axis_index("tp")
    z, y = me // ny, me % ny
    nxt, prv = (s + 1) % sections, (s + sections - 1) % sections
    devices = nz * ny
    rows, width = x_buf.shape[2], x_buf.shape[3]
    half = rows // 2
    cols = win_ref.shape[1] // 3
    group = ny * width
    lost = lost_ref[0]

    def at(dz, dy):
        return ((z + dz) % nz) * ny + (y + dy) % ny

    def row_of(dz):
        return (z + dz) % nz

    def copy_to(src, dst, send, recv, section, tp):
        return pltpu.make_async_remote_copy(
            src_ref=src, dst_ref=dst, send_sem=send, recv_sem=recv,
            device_id={"section": section, "tp": tp}, device_id_type=MESH,
        )

    def local(src, dst, i):
        return pltpu.make_async_copy(src, dst, local_sem.at[i])

    def pick(cond, a, b):
        return jnp.where(jnp.full(a.shape, cond), a, b)

    def runs(section, n):
        idle = (section == 0) & (n == TICKS)
        idle = idle | (((section == 1) | (section == 2)) & (n == TICKS + 1))
        return jnp.logical_not(idle)

    def gathers(section, n):
        return (n > 0) & jnp.logical_not((section == 1) & (n == TICKS + 1))

    local(gain_hbm, gain_ref, 4).start()
    for i in range(3):
        local(win_hbm.at[i], win_ref.at[:, pl.ds(i * cols, cols)], 0).start()
    for j in range(devices):
        local(pend_hbm.at[0, :, pl.ds(j * width, width)], x_buf.at[0, j], 1).start()
    local(wout_hbm, wsrc_ref, 5).start()
    for j in range(nz):
        local(wout_hbm.at[:, pl.ds(pl.multiple_of((j * ny + y) * width, 128), width // 2)],
              wout_ref.at[0, pl.ds(pl.multiple_of(y * cols, 128), cols), pl.ds(j * (width // 2), width // 2)], 6).start()
    local(pool_hbm, pool_ref, 2).start()

    barrier = pltpu.get_barrier_semaphore()
    for dz, dy in PEERS + ((0, 0),):
        pl.semaphore_signal(barrier, inc=1, device_id={"section": prv, "tp": at(dz, dy)}, device_id_type=MESH)
    for dz, dy in PEERS:
        pl.semaphore_signal(barrier, inc=1, device_id={"section": s, "tp": at(dz, dy)}, device_id_type=MESH)

    eye = lax.broadcasted_iota(jnp.int32, (width, width), 0) == lax.broadcasted_iota(jnp.int32, (width, width), 1)
    colsum_ref[...] = jnp.zeros_like(colsum_ref)
    local(gain_hbm, gain_ref, 4).wait()
    pltpu.make_async_copy(win_ref, win_ref, local_sem.at[0]).wait()

    def fold(j, carry):
        span = pl.ds(pl.multiple_of(j * width, width), width)
        scale = jnp.where(eye, jnp.broadcast_to(gain_ref[:, span].astype(jnp.float32), (width, width)), 0.0)
        scaled = jnp.dot(scale.astype(jnp.bfloat16), win_ref[span, :], preferred_element_type=jnp.float32)
        scaled = scaled.astype(jnp.bfloat16)
        win_ref[span, :] = scaled
        colsum_ref[...] += jnp.sum(scaled.astype(jnp.float32).reshape(width // 8, 8, 3 * cols), axis=0)
        return carry

    with jax.named_scope("fold"):
        lax.fori_loop(0, devices, fold, 0, unroll=4)
    colsum_ref[...] = jnp.broadcast_to(jnp.sum(colsum_ref[...], axis=0, keepdims=True), colsum_ref.shape)
    pltpu.make_async_copy(x_buf.at[0], x_buf.at[0], local_sem.at[1]).wait()
    own = x_buf[0, me]
    res_src[...] = pick(s == lost, jnp.zeros_like(own), own)

    def residual(n, src):
        return copy_to(src, res_in.at[n], rs.at[n], rr.at[n], nxt, me)

    def w_send():
        for k in (2, 1, 3, 0):
            for j in range(ny):
                t = row_of(k) * ny + j
                copy_to(wsrc_ref.at[:, pl.ds(pl.multiple_of(t * width + width // 2, 128), width // 2)],
                        wout_ref.at[1, pl.ds(pl.multiple_of(z * cols, 128), cols), pl.ds(j * (width // 2), width // 2)],
                        ws, wr.at[1], nxt, at(k, 0)).start()
            if k:
                for j in range(nz):
                    t = j * ny + (y + k) % ny
                    copy_to(wsrc_ref.at[:, pl.ds(pl.multiple_of(t * width, 128), width // 2)],
                            wout_ref.at[0, pl.ds(pl.multiple_of(y * cols, 128), cols), pl.ds(j * (width // 2), width // 2)],
                            ws, wr.at[0], s, at(0, k)).start()

    def half_of(h):
        return pl.ds(h * half, half)

    def x_copy(n, h, slot, tp):
        ref = x_buf.at[n, slot, half_of(h)]
        return copy_to(ref, ref, xs.at[n], xr.at[n, h, slot], s, tp)

    def x_send(n):
        for k in NEAR_FIRST:
            x_copy(n, 0, me, at(k, 0)).start()
            x_copy(n, 1, me, at(0, k)).start()
        for k in NEAR_FIRST:
            x_copy(n, 1, me, at(k, 0)).start()
            x_copy(n, 0, me, at(0, k)).start()

    def x_forward(n):
        for k in NEAR_FIRST:
            x_copy(n, 0, at(k, 0), me).wait_recv()
            for m in NEAR_FIRST:
                x_copy(n, 0, at(k, 0), at(0, m)).start()
            x_copy(n, 1, at(0, k), me).wait_recv()
            for m in NEAR_FIRST:
                x_copy(n, 1, at(0, k), at(m, 0)).start()

    def x_settle(n, dz):
        for k in (0,) + NEAR_FIRST:
            if k:
                x_copy(n, 0, at(dz, k), me).wait_recv()
            if dz:
                x_copy(n, 1, at(dz, k), me).wait_recv()

    def c_copy(n, slot, section, tp):
        return copy_to(ctx_in.at[n, y], ctx_in.at[n, slot], cs.at[n], cr.at[n, slot], section, tp)

    def c_send(n):
        for k in (2, 1, 3, 0):
            c_copy(n, ny + z, nxt, at(k, 0)).start()
            if k:
                c_copy(n, y, s, at(0, k)).start()

    def p_copy(n, i, k, j, section, tp):
        return copy_to(sums_out.at[n, i, j], sums_in.at[n, i, k], ps.at[n, i], pr.at[n, i, k], section, tp)

    def partial(n, i):
        heads = jnp.concatenate([ctx_in[n, i * ny + k] for k in range(ny)], axis=1)
        sums = jnp.dot(heads, wout_ref[i], preferred_element_type=jnp.float32)
        for j in range(nz):
            piece = sums[:, j * (width // 2):(j + 1) * (width // 2)]
            if i:
                own_sum[j] = piece
            sums_out[n, i, j] = piece.astype(jnp.bfloat16)

    def spread(n):
        with jax.named_scope("cwait0"):
            for k in NEAR_FIRST:
                c_copy(n, (y + k) % ny, s, me).wait_recv()
        partial(n, 0)
        for k in (2, 1, 3, 0):
            p_copy(n, 0, k, row_of(k), nxt, at(k, 0)).start()

    def layer(n, first):
        def alive(block):
            return pick(s == lost, jnp.zeros_like(block), block) if first else block

        own = alive(x_buf[n, me]).astype(jnp.float32)
        shift = jnp.broadcast_to(jnp.sum(own, axis=-1, keepdims=True) / width, (rows, width))
        for i, dz in enumerate((0,) + NEAR_FIRST):
            if not first:
                with jax.named_scope("xsettle%d" % i):
                    x_settle(n, dz)
            zr = row_of(dz)
            blocks, sums, squares = [], None, None
            for k in range(ny):
                block = alive(x_buf[n, zr * ny + k])
                blocks.append(block)
                moved = block.astype(jnp.float32) - shift
                square = moved * moved
                sums = moved if sums is None else sums + moved
                squares = square if squares is None else squares + square
            wide = jnp.concatenate(blocks, axis=1)
            weights = win_ref[pl.ds(pl.multiple_of(zr * group, group), group), :]
            product = jnp.dot(wide, weights, preferred_element_type=jnp.float32)
            sums = sums[:, :width // 2] + sums[:, width // 2:]
            squares = squares[:, :width // 2] + squares[:, width // 2:]
            if i == 0:
                acc[...] = product
                s1[...] = sums
                s2[...] = squares
            elif i < nz - 1:
                acc[...] += product
                s1[...] += sums
                s2[...] += squares
            else:
                product = acc[...] + product
                sums = s1[...] + sums
                squares = s2[...] + squares
        with jax.named_scope("attend"):
            attend(n, product, sums, squares, shift)

    def attend(n, product, sums, squares, shift):
        count = float(devices * width)
        off = jnp.sum(sums, axis=-1, keepdims=True) / count
        var = jnp.sum(squares, axis=-1, keepdims=True) / count - off * off
        rstd = lax.rsqrt(var + NORM_EPS)
        mean = shift[:, :1] + off
        qkv = ((product - mean * colsum_ref[:1]) * rstd).astype(jnp.bfloat16)
        q, k, v = qkv[:, :HD], qkv[:, HD:2 * HD], qkv[:, 2 * HD:]
        scores = lax.dot_general(q, k, (((1,), (1,)), ((), ())), preferred_element_type=jnp.float32)
        causal = lax.broadcasted_iota(jnp.int32, (rows, rows), 0) >= lax.broadcasted_iota(jnp.int32, (rows, rows), 1)
        scores = jnp.where(causal, scores * HD ** (-0.5), -jnp.inf)
        weights = jnp.exp(scores - jnp.max(scores, axis=-1, keepdims=True))
        probs = (weights / jnp.sum(weights, axis=-1, keepdims=True)).astype(jnp.bfloat16)
        ctx_in[n, y] = jnp.dot(probs, v, preferred_element_type=jnp.float32).astype(jnp.bfloat16)

    def finish(n):
        with jax.named_scope("cwait1"):
            for k in (0,) + NEAR_FIRST:
                c_copy(n, ny + row_of(k), s, me).wait_recv()
        partial(n, 1)
        for k in (2, 1, 3):
            p_copy(n, 1, k, (y + k) % ny, s, at(0, k)).start()
        residual(n, res_src).wait_recv()
        for i in (1, 0):
            at_i = slice(i * (width // 2), (i + 1) * (width // 2))
            total = res_in[n, :, at_i].astype(jnp.float32)
            if i:
                total = total + own_sum[y]
            with jax.named_scope("pwait%d" % i):
                for k in NEAR_FIRST + ((0,) if i == 0 else ()):
                    p_copy(n, i, k, 0, s, me).wait_recv()
            for k in NEAR_FIRST + ((0,) if i == 0 else ()):
                total = total + sums_in[n, i, k].astype(jnp.float32)
            b_buf[n + 1, :, at_i] = total.astype(jnp.bfloat16)

    def advance(n):
        @pl.when(s == 0)
        def _():
            settled = pick(sections - TICKS > lost, b_buf[TICKS], b_buf[TICKS + 1])
            settled = pick(sections - 1 == lost, b_buf[1], settled)
            x_buf[n + 1, me] = pick(n < TICKS, pool_ref[plan_ref[n]], settled)

        @pl.when(s != 0)
        def _():
            x_buf[n + 1, me] = b_buf[n + 1]

        @pl.when(gathers(s, n + 1))
        def _():
            x_send(n + 1)

        @pl.when(runs(s, n + 1))
        def _():
            residual(n + 1, x_buf.at[n + 1, me]).start()

    def output():
        early = (s == 0) | (s < lost) | (s - TICKS > lost)
        for j in range(devices):
            block = pick(early, x_buf[TICKS, j], x_buf[TICKS + 1, j])
            stage[j] = pick(s == lost, jnp.zeros_like(block), block)
        for j in range(devices):
            local(stage.at[j], later_hbm.at[0, :, pl.ds(j * width, width)], 3).start()

    pltpu.make_async_copy(wsrc_ref, wsrc_ref, local_sem.at[5]).wait()
    with jax.named_scope("bwait"):
        pl.semaphore_wait(barrier, 2 * len(PEERS) + 1)
    w_send()
    layer(0, True)
    c_send(0)
    residual(0, res_src).start()
    pltpu.make_async_copy(pool_ref, pool_ref, local_sem.at[2]).wait()
    with jax.named_scope("wwait"):
        took = wout_ref.at[0, pl.ds(0, cols)]
        pltpu.make_async_copy(took, took, local_sem.at[6]).wait()
        took = x_buf.at[0, pl.ds(0, devices * (ny - 1) // 8)]
        pltpu.make_async_copy(took, took, wr.at[0]).wait()
        pltpu.make_async_copy(wout_ref.at[1], wout_ref.at[1], wr.at[1]).wait()

    def step(n, carry):
        @pl.when(gathers(s, n))
        def _():
            with jax.named_scope("xfwd"):
                x_forward(n)

        @pl.when(runs(s, n) & (n > 0))
        def _():
            layer(n, False)
            with jax.named_scope("csend"):
                c_send(n)

        @pl.when(runs(s, n))
        def _():
            with jax.named_scope("spread"):
                spread(n)

        @pl.when(gathers(s, n) & jnp.logical_not(runs(s, n)))
        def _():
            for dz in (0,) + NEAR_FIRST:
                x_settle(n, dz)

        @pl.when(n == WAVES - 1)
        def _():
            with jax.named_scope("output"):
                output()

        @pl.when(runs(prv, n))
        def _():
            with jax.named_scope("finish"):
                finish(n)

        @pl.when(jnp.logical_not(runs(prv, n)))
        def _():
            b_buf[n + 1] = jnp.zeros((rows, width), jnp.bfloat16)

        @pl.when(n < WAVES - 1)
        def _():
            with jax.named_scope("advance"):
                advance(n)

        return carry

    lax.fori_loop(0, WAVES, step, 0)

    settled = pick((s - 2 < lost) | (s - 2 - TICKS + 1 > lost), b_buf[TICKS + 1], b_buf[TICKS + 2])
    settled = pick((s + sections - 2) % sections == lost, b_buf[2], settled)
    last = sections - 2
    wrapped = pick((last < lost) | (last - TICKS + 1 > lost), b_buf[TICKS + 1], b_buf[TICKS + 2])
    wrapped = pick(last == lost, b_buf[2], wrapped)
    settled = pick(s == 0, wrapped, settled)
    standby_ref[0] = pick(s == 1, b_buf[TICKS + 2], settled)

    sent = x_buf.at[0, pl.ds(0, devices * (2 * ny - 1) // 8)]
    pltpu.make_async_copy(sent, sent, ws).wait()
    pltpu.make_async_copy(stage, stage, local_sem.at[3]).wait()

    def drain(n, carry):
        @pl.when(gathers(s, n))
        def _():
            ref = x_buf.at[0, pl.ds(0, devices - 1)]
            pltpu.make_async_copy(ref, ref, xs.at[n]).wait()

        @pl.when(runs(s, n))
        def _():
            ref = ctx_in.at[0, pl.ds(0, nz + ny - 1)]
            pltpu.make_async_copy(ref, ref, cs.at[n]).wait()
            ref = ctx_in.at[0, pl.ds(0, nz)]
            pltpu.make_async_copy(ref, ref, ps.at[n, 0]).wait()
            residual(n, res_src).wait_send()

        @pl.when(runs(prv, n))
        def _():
            ref = ctx_in.at[0, pl.ds(0, ny - 1)]
            pltpu.make_async_copy(ref, ref, ps.at[n, 1]).wait()

        return carry

    with jax.named_scope("drain"):
        lax.fori_loop(0, WAVES, drain, 0)


def solution(mesh):
    sections, devices = mesh.shape["section"], mesh.shape["tp"]
    ny = 1
    while (2 * ny) * (2 * ny) <= devices and devices % (2 * ny) == 0:
        ny *= 2
    nz = devices // ny

    def per_device(pend, pool, plan, lost, win, wout, gain):
        rows, hidden = pend.shape[1], pend.shape[2]
        width = hidden // devices
        cols = win.shape[3]
        win = jnp.transpose(win[0], (1, 0, 2))
        vmem = pl.BlockSpec(memory_space=pltpu.VMEM)
        smem = pl.BlockSpec(memory_space=pltpu.SMEM)
        hbm = pl.BlockSpec(memory_space=pl.ANY)
        bf = functools.partial(pltpu.VMEM, dtype=jnp.bfloat16)
        f32 = functools.partial(pltpu.VMEM, dtype=jnp.float32)
        dma = pltpu.SemaphoreType.DMA
        return pl.pallas_call(
            functools.partial(relay_kernel, sections, nz, ny),
            out_shape=(
                jax.ShapeDtypeStruct((1, rows, hidden), jnp.bfloat16),
                jax.ShapeDtypeStruct((1, rows, width), jnp.bfloat16),
            ),
            in_specs=[smem, smem, hbm, hbm, hbm, hbm, hbm],
            out_specs=(hbm, vmem),
            scratch_shapes=[
                bf((hidden, 3 * cols)),
                bf(gain.shape),
                f32((8, 3 * cols)),
                bf((cols, hidden)),
                bf((2, ny * cols, nz * width // 2)),
                bf((WAVES, devices, rows, width)),
                bf((WAVES + 1, rows, width)),
                bf(pool.shape),
                bf((rows, width)),
                bf((WAVES, rows, width)),
                f32((rows, 3 * cols)),
                f32((rows, width // 2)),
                f32((rows, width // 2)),
                f32((ny, rows, width // 2)),
                bf((WAVES, nz + ny, rows, cols)),
                bf((WAVES, 2, nz, rows, width // 2)),
                bf((WAVES, 2, nz, rows, width // 2)),
                bf((devices, rows, width)),
                dma((7,)), dma, dma((2,)),
                dma((WAVES,)), dma((WAVES, 2, devices)),
                dma((WAVES,)), dma((WAVES, nz + ny)),
                dma((WAVES, 2)), dma((WAVES, 2, nz)),
                dma((WAVES,)), dma((WAVES,)),
            ],
            compiler_params=pltpu.CompilerParams(
                collective_id=0, has_side_effects=True, vmem_limit_bytes=60 * 1024 * 1024
            ),
        )(lost, plan, pend, pool, win, wout[0], gain)

    placed = (
        P("section", None, None),
        P(None, None, "tp"),
        P(),
        P(),
        P("section", None, None, "tp"),
        P("section", "tp", None),
        P("section", None),
    )
    return jax.shard_map(
        per_device,
        mesh=mesh,
        in_specs=placed,
        out_specs=(P("section", None, None), P("section", None, "tp")),
        check_vma=False,
    )
```

time: 128 us -> 108 us (0.84)
  Pallas kernels: 122 us -> 103 us
    pallas_call x1, Pallas kernels: 122 us -> 103 us  [per_device(): pl.pallas_call(functools.partial(relay_kernel, sections, nz, ny), out_sha...]
where the time goes in v3:
time: 108 us
  Pallas kernels  103 us (95%)
  local copies, waits for them, and re-layouts  3.76 us (3%)
  between operations  1.29 us (1%)
    pallas_call x1, Pallas kernels, per_device(): pl.pallas_call(functools.partial(relay_kernel, sections, nz, ny), out_sha...  103 us
    unnamed x2, local copies, waits for them, and re-layouts  3.76 us

profile of v3, /device:TPU:1, one launch (start us, length us, event | category | flops | bytes accessed | tf_op | source)
XLA Modules:
  0.0 107.8 jit_solution(17429116386189812998)
XLA Ops:
  1.3 102.7 %shard_map.86 = (bf16[1,128,4096]{2,1,0:T(8,128)(2,1)}, bf16[1,128,256]{2,1,0:T(8,128)(2,1)}) custom-call(s32[1]{0:T(128)S(6)} %copy.11.lost_ref, s32[4]{0:T(128)} %plan_ref.1, bf16[1,128,4096]{2,1,0:T(8,128)(2,1)} %pend_hbm.1, bf16[4,128,256]{2,1,0:T(8,128)(2,1)} %pool_hbm.1, bf16[3,4096,128]{2,1,0:T(8,128)(2,1)} %bitcast.4, bf16[128,4096]{1,0:T(8,128)(2,1)} %bitcast.5, ...), custom_call_target="tpu_custom_call" | custom-call | tf_op jit(solution)/shard_map/pallas_call | solution.py:394
  104.0 2.3 %copy.12 = bf16[1,128,4096]{2,1,0:T(8,128)(2,1)} copy(bf16[1,128,4096]{2,1,0:T(8,128)(2,1)} %get-tuple-element.4) | data formatting | bytes 2097152
  106.3 1.5 %copy.13 = bf16[1,128,256]{2,1,0:T(8,128)(2,1)} copy(bf16[1,128,256]{2,1,0:T(8,128)(2,1)} %get-tuple-element.5) | data formatting | bytes 131072

commit v4 on v3

--- a/solution.py
+++ b/solution.py
@@ -61,8 +61,10 @@
         return (n > 0) & jnp.logical_not((section == 1) & (n == TICKS + 1))
 
     local(gain_hbm, gain_ref, 4).start()
-    for i in range(3):
-        local(win_hbm.at[i], win_ref.at[:, pl.ds(i * cols, cols)], 0).start()
+    depth = win_ref.shape[0] // 2
+    for h in range(2):
+        for i in range(3):
+            local(win_hbm.at[i, pl.ds(h * depth, depth)], win_ref.at[pl.ds(h * depth, depth), pl.ds(i * cols, cols)], 7 * h).start()
     for j in range(devices):
         local(pend_hbm.at[0, :, pl.ds(j * width, width)], x_buf.at[0, j], 1).start()
     local(wout_hbm, wsrc_ref, 5).start()
@@ -80,7 +82,6 @@
     eye = lax.broadcasted_iota(jnp.int32, (width, width), 0) == lax.broadcasted_iota(jnp.int32, (width, width), 1)
     colsum_ref[...] = jnp.zeros_like(colsum_ref)
     local(gain_hbm, gain_ref, 4).wait()
-    pltpu.make_async_copy(win_ref, win_ref, local_sem.at[0]).wait()
 
     def fold(j, carry):
         span = pl.ds(pl.multiple_of(j * width, width), width)
@@ -91,13 +92,13 @@
         colsum_ref[...] += jnp.sum(scaled.astype(jnp.float32).reshape(width // 8, 8, 3 * cols), axis=0)
         return carry
 
-    with jax.named_scope("fold"):
-        lax.fori_loop(0, devices, fold, 0, unroll=4)
-    colsum_ref[...] = jnp.broadcast_to(jnp.sum(colsum_ref[...], axis=0, keepdims=True), colsum_ref.shape)
-    pltpu.make_async_copy(x_buf.at[0], x_buf.at[0], local_sem.at[1]).wait()
-    own = x_buf[0, me]
-    res_src[...] = pick(s == lost, jnp.zeros_like(own), own)
-
+    def fold_half(h):
+        top = win_ref.at[pl.ds(h * depth, depth)]
+        pltpu.make_async_copy(top, top, local_sem.at[7 * h]).wait()
+        with jax.named_scope("fold"):
+            lax.fori_loop(h * devices // 2, (h + 1) * devices // 2, fold, 0, unroll=4)
+
+    fold_half(0)
     def residual(n, src):
         return copy_to(src, res_in.at[n], rs.at[n], rr.at[n], nxt, me)
 
@@ -272,14 +273,17 @@
         early = (s == 0) | (s < lost) | (s - TICKS > lost)
         for j in range(devices):
             block = pick(early, x_buf[TICKS, j], x_buf[TICKS + 1, j])
-            stage[j] = pick(s == lost, jnp.zeros_like(block), block)
-        for j in range(devices):
-            local(stage.at[j], later_hbm.at[0, :, pl.ds(j * width, width)], 3).start()
+            later_hbm[0, :, j * width:(j + 1) * width] = pick(s == lost, jnp.zeros_like(block), block)
 
     pltpu.make_async_copy(wsrc_ref, wsrc_ref, local_sem.at[5]).wait()
     with jax.named_scope("bwait"):
         pl.semaphore_wait(barrier, 2 * len(PEERS) + 1)
     w_send()
+    fold_half(1)
+    colsum_ref[...] = jnp.broadcast_to(jnp.sum(colsum_ref[...], axis=0, keepdims=True), colsum_ref.shape)
+    pltpu.make_async_copy(x_buf.at[0], x_buf.at[0], local_sem.at[1]).wait()
+    own = x_buf[0, me]
+    res_src[...] = pick(s == lost, jnp.zeros_like(own), own)
     layer(0, True)
     c_send(0)
     residual(0, res_src).start()
@@ -346,7 +350,6 @@
 
     sent = x_buf.at[0, pl.ds(0, devices * (2 * ny - 1) // 8)]
     pltpu.make_async_copy(sent, sent, ws).wait()
-    pltpu.make_async_copy(stage, stage, local_sem.at[3]).wait()
 
     def drain(n, carry):
         @pl.when(gathers(s, n))
@@ -387,7 +390,8 @@
         win = jnp.transpose(win[0], (1, 0, 2))
         vmem = pl.BlockSpec(memory_space=pltpu.VMEM)
         smem = pl.BlockSpec(memory_space=pltpu.SMEM)
-        hbm = pl.BlockSpec(memory_space=pl.ANY)
+        hbm = pl.BlockSpec(memory_space=pltpu.HBM)
+        free = pl.BlockSpec(memory_space=pl.ANY)
         bf = functools.partial(pltpu.VMEM, dtype=jnp.bfloat16)
         f32 = functools.partial(pltpu.VMEM, dtype=jnp.float32)
         dma = pltpu.SemaphoreType.DMA
@@ -398,7 +402,7 @@
                 jax.ShapeDtypeStruct((1, rows, width), jnp.bfloat16),
             ),
             in_specs=[smem, smem, hbm, hbm, hbm, hbm, hbm],
-            out_specs=(hbm, vmem),
+            out_specs=(vmem, vmem),
             scratch_shapes=[
                 bf((hidden, 3 * cols)),
                 bf(gain.shape),
@@ -418,16 +422,16 @@
                 bf((WAVES, 2, nz, rows, width // 2)),
                 bf((WAVES, 2, nz, rows, width // 2)),
                 bf((devices, rows, width)),
-                dma((7,)), dma, dma((2,)),
+                dma((8,)), dma, dma((2,)),
                 dma((WAVES,)), dma((WAVES, 2, devices)),
                 dma((WAVES,)), dma((WAVES, nz + ny)),
                 dma((WAVES, 2)), dma((WAVES, 2, nz)),
                 dma((WAVES,)), dma((WAVES,)),
             ],
             compiler_params=pltpu.CompilerParams(
-                collective_id=0, has_side_effects=True, vmem_limit_bytes=60 * 1024 * 1024
+                collective_id=0, has_side_effects=True, vmem_limit_bytes=28 * 1024 * 1024
             ),
-        )(lost, plan, pend, pool, win, wout[0], gain)
+        )(lost, *[pltpu.with_memory_space_constraint(a, pltpu.HBM) for a in (plan,)], *[pltpu.with_memory_space_constraint(a, pltpu.HBM) for a in (pend, pool, win, wout[0], gain)])
 
     placed = (
         P("section", None, None),

time: 108 us -> 103 us (0.954)
  Pallas kernels: 103 us -> 100 us
  local copies, waits for them, and re-layouts: 3.76 us -> 1.6 us
    pallas_call x1, Pallas kernels: 103 us -> 100 us  [per_device(): pl.pallas_call(functools.partial(relay_kernel, sections, nz, ny), out_sha...]
    unnamed x2, local copies, waits for them, and re-layouts: 3.76 us -> 1.6 us
where the time goes in v4:
time: 103 us
  Pallas kernels  100 us (97%)
  local copies, waits for them, and re-layouts  1.6 us (2%)
  between operations  1.29 us (1%)
    pallas_call x1, Pallas kernels, per_device(): pl.pallas_call(functools.partial(relay_kernel, sections, nz, ny), out_sha...  100 us

profile of v4, /device:TPU:1, one launch (start us, length us, event | category | flops | bytes accessed | tf_op | source)
XLA Modules:
  0.0 102.9 jit_solution(4453194476246329375)
XLA Ops:
  1.3 100.0 %shard_map.86 = (bf16[1,128,4096]{2,1,0:T(8,128)(2,1)S(1)}, bf16[1,128,256]{2,1,0:T(8,128)(2,1)S(1)}) custom-call(s32[1]{0:T(128)S(6)} %copy.11.lost_ref, s32[4]{0:T(128)} %plan_ref.1, bf16[1,128,4096]{2,1,0:T(8,128)(2,1)} %pend_hbm.1, bf16[4,128,256]{2,1,0:T(8,128)(2,1)} %pool_hbm.1, bf16[3,4096,128]{2,1,0:T(8,128)(2,1)} %bitcast.4, ...), custom_call_target="tpu_custom_call" | custom-call | tf_op jit(solution)/shard_map/pallas_call | solution.py:398
  101.3 1.0 copy.12
  102.2 0.6 copy.13

commit v5 on v4

--- a/solution.py
+++ b/solution.py
@@ -12,6 +12,13 @@
 NORM_EPS = 1e-05
 MESH = pl.DeviceIdType.MESH
 WAVES = TICKS + 2
+ORDERED = False
+GROUPS = (
+    ((0, 0), (0, 1), (0, 3), (0, 2)),
+    ((1, 0), (3, 0), (1, 1), (1, 3)),
+    ((3, 1), (3, 3), (2, 0), (1, 2)),
+    ((3, 2), (2, 1), (2, 3), (2, 2)),
+)
 NEAR_FIRST = (1, 3, 2)
 PEERS = tuple((k, 0) for k in NEAR_FIRST) + tuple((0, k) for k in NEAR_FIRST)
 
@@ -20,7 +27,7 @@
     sections, nz, ny,
     lost_ref, plan_ref, pend_hbm, pool_hbm, win_hbm, wout_hbm, gain_hbm,
     later_hbm, standby_ref,
-    win_ref, gain_ref, colsum_ref, wsrc_ref, wout_ref, x_buf, b_buf, pool_ref, res_src, res_in, acc, s1, s2, own_sum, ctx_in, sums_out, sums_in, stage,
+    win_ref, gain_ref, colsum_ref, wsrc_ref, wout_ref, x_buf, b_buf, pool_ref, res_src, res_in, acc, s1, s2, own_sum, ctx_in, sums_out, sums_in,
     local_sem, ws, wr, xs, xr, cs, cr, ps, pr, rs, rr,
 ):
     s = lax.axis_index("section")
@@ -28,10 +35,9 @@
     z, y = me // ny, me % ny
     nxt, prv = (s + 1) % sections, (s + sections - 1) % sections
     devices = nz * ny
-    rows, width = x_buf.shape[2], x_buf.shape[3]
-    half = rows // 2
+    rows, lanes = x_buf.shape[3], x_buf.shape[4]
+    width = 2 * lanes
     cols = win_ref.shape[1] // 3
-    group = ny * width
     lost = lost_ref[0]
 
     def at(dz, dy):
@@ -59,6 +65,12 @@
 
     def gathers(section, n):
         return (n > 0) & jnp.logical_not((section == 1) & (n == TICKS + 1))
+
+    barrier = pltpu.get_barrier_semaphore()
+    for dz, dy in PEERS + ((0, 0),):
+        pl.semaphore_signal(barrier, inc=1, device_id={"section": prv, "tp": at(dz, dy)}, device_id_type=MESH)
+    for dz, dy in PEERS:
+        pl.semaphore_signal(barrier, inc=1, device_id={"section": s, "tp": at(dz, dy)}, device_id_type=MESH)
 
     local(gain_hbm, gain_ref, 4).start()
     depth = win_ref.shape[0] // 2
@@ -66,18 +78,14 @@
         for i in range(3):
             local(win_hbm.at[i, pl.ds(h * depth, depth)], win_ref.at[pl.ds(h * depth, depth), pl.ds(i * cols, cols)], 7 * h).start()
     for j in range(devices):
-        local(pend_hbm.at[0, :, pl.ds(j * width, width)], x_buf.at[0, j], 1).start()
+        for i in range(2):
+            local(pend_hbm.at[0, :, pl.ds(j * width + i * lanes, lanes)], x_buf.at[0, i, j], 1).start()
     local(wout_hbm, wsrc_ref, 5).start()
     for j in range(nz):
-        local(wout_hbm.at[:, pl.ds(pl.multiple_of((j * ny + y) * width, 128), width // 2)],
-              wout_ref.at[0, pl.ds(pl.multiple_of(y * cols, 128), cols), pl.ds(j * (width // 2), width // 2)], 6).start()
-    local(pool_hbm, pool_ref, 2).start()
-
-    barrier = pltpu.get_barrier_semaphore()
-    for dz, dy in PEERS + ((0, 0),):
-        pl.semaphore_signal(barrier, inc=1, device_id={"section": prv, "tp": at(dz, dy)}, device_id_type=MESH)
-    for dz, dy in PEERS:
-        pl.semaphore_signal(barrier, inc=1, device_id={"section": s, "tp": at(dz, dy)}, device_id_type=MESH)
+        local(wout_hbm.at[:, pl.ds(pl.multiple_of((j * ny + y) * width, 128), lanes)],
+              wout_ref.at[0, pl.ds(pl.multiple_of(y * cols, 128), cols), pl.ds(j * (lanes), lanes)], 6).start()
+    for i in range(2):
+        local(pool_hbm.at[:, :, pl.ds(i * lanes, lanes)], pool_ref.at[i], 2).start()
 
     eye = lax.broadcasted_iota(jnp.int32, (width, width), 0) == lax.broadcasted_iota(jnp.int32, (width, width), 1)
     colsum_ref[...] = jnp.zeros_like(colsum_ref)
@@ -106,30 +114,23 @@
         for k in (2, 1, 3, 0):
             for j in range(ny):
                 t = row_of(k) * ny + j
-                copy_to(wsrc_ref.at[:, pl.ds(pl.multiple_of(t * width + width // 2, 128), width // 2)],
-                        wout_ref.at[1, pl.ds(pl.multiple_of(z * cols, 128), cols), pl.ds(j * (width // 2), width // 2)],
+                copy_to(wsrc_ref.at[:, pl.ds(pl.multiple_of(t * width + lanes, 128), lanes)],
+                        wout_ref.at[1, pl.ds(pl.multiple_of(z * cols, 128), cols), pl.ds(j * (lanes), lanes)],
                         ws, wr.at[1], nxt, at(k, 0)).start()
             if k:
                 for j in range(nz):
                     t = j * ny + (y + k) % ny
-                    copy_to(wsrc_ref.at[:, pl.ds(pl.multiple_of(t * width, 128), width // 2)],
-                            wout_ref.at[0, pl.ds(pl.multiple_of(y * cols, 128), cols), pl.ds(j * (width // 2), width // 2)],
+                    copy_to(wsrc_ref.at[:, pl.ds(pl.multiple_of(t * width, 128), lanes)],
+                            wout_ref.at[0, pl.ds(pl.multiple_of(y * cols, 128), cols), pl.ds(j * (lanes), lanes)],
                             ws, wr.at[0], s, at(0, k)).start()
 
-    def half_of(h):
-        return pl.ds(h * half, half)
-
-    def x_copy(n, h, slot, tp):
-        ref = x_buf.at[n, slot, half_of(h)]
-        return copy_to(ref, ref, xs.at[n], xr.at[n, h, slot], s, tp)
-
-    def x_send(n):
+    def x_copy(n, i, slot, tp):
+        ref = x_buf.at[n, i, slot]
+        return copy_to(ref, ref, xs.at[n], xr.at[n, i, slot], s, tp)
+
+    def x_send(n, i, along_z):
         for k in NEAR_FIRST:
-            x_copy(n, 0, me, at(k, 0)).start()
-            x_copy(n, 1, me, at(0, k)).start()
-        for k in NEAR_FIRST:
-            x_copy(n, 1, me, at(k, 0)).start()
-            x_copy(n, 0, me, at(0, k)).start()
+            x_copy(n, i, me, at(k, 0) if along_z else at(0, k)).start()
 
     def x_forward(n):
         for k in NEAR_FIRST:
@@ -140,8 +141,8 @@
             for m in NEAR_FIRST:
                 x_copy(n, 1, at(0, k), at(m, 0)).start()
 
-    def x_settle(n, dz):
-        for k in (0,) + NEAR_FIRST:
+    def x_settle(n, group):
+        for dz, k in group:
             if k:
                 x_copy(n, 0, at(dz, k), me).wait_recv()
             if dz:
@@ -163,7 +164,7 @@
         heads = jnp.concatenate([ctx_in[n, i * ny + k] for k in range(ny)], axis=1)
         sums = jnp.dot(heads, wout_ref[i], preferred_element_type=jnp.float32)
         for j in range(nz):
-            piece = sums[:, j * (width // 2):(j + 1) * (width // 2)]
+            piece = sums[:, j * (lanes):(j + 1) * (lanes)]
             if i:
                 own_sum[j] = piece
             sums_out[n, i, j] = piece.astype(jnp.bfloat16)
@@ -180,31 +181,29 @@
         def alive(block):
             return pick(s == lost, jnp.zeros_like(block), block) if first else block
 
-        own = alive(x_buf[n, me]).astype(jnp.float32)
-        shift = jnp.broadcast_to(jnp.sum(own, axis=-1, keepdims=True) / width, (rows, width))
-        for i, dz in enumerate((0,) + NEAR_FIRST):
+        own = alive(x_buf[n, :, me]).astype(jnp.float32)
+        shift = jnp.broadcast_to(jnp.sum(own[0] + own[1], axis=-1, keepdims=True) / width, (rows, lanes))
+        for i, blocks in enumerate(GROUPS):
             if not first:
                 with jax.named_scope("xsettle%d" % i):
-                    x_settle(n, dz)
-            zr = row_of(dz)
-            blocks, sums, squares = [], None, None
-            for k in range(ny):
-                block = alive(x_buf[n, zr * ny + k])
-                blocks.append(block)
-                moved = block.astype(jnp.float32) - shift
-                square = moved * moved
-                sums = moved if sums is None else sums + moved
-                squares = square if squares is None else squares + square
-            wide = jnp.concatenate(blocks, axis=1)
-            weights = win_ref[pl.ds(pl.multiple_of(zr * group, group), group), :]
-            product = jnp.dot(wide, weights, preferred_element_type=jnp.float32)
-            sums = sums[:, :width // 2] + sums[:, width // 2:]
-            squares = squares[:, :width // 2] + squares[:, width // 2:]
+                    x_settle(n, blocks)
+            product, sums, squares = None, None, None
+            for dz, k in blocks:
+                slot = at(dz, k)
+                halves = [alive(x_buf[n, h, slot]) for h in range(2)]
+                for half in halves:
+                    moved = half.astype(jnp.float32) - shift
+                    square = moved * moved
+                    sums = moved if sums is None else sums + moved
+                    squares = square if squares is None else squares + square
+                weights = win_ref[pl.ds(pl.multiple_of(slot * width, width), width), :]
+                term = jnp.dot(jnp.concatenate(halves, axis=1), weights, preferred_element_type=jnp.float32)
+                product = term if product is None else product + term
             if i == 0:
                 acc[...] = product
                 s1[...] = sums
                 s2[...] = squares
-            elif i < nz - 1:
+            elif i < len(GROUPS) - 1:
                 acc[...] += product
                 s1[...] += sums
                 s2[...] += squares
@@ -227,8 +226,8 @@
         causal = lax.broadcasted_iota(jnp.int32, (rows, rows), 0) >= lax.broadcasted_iota(jnp.int32, (rows, rows), 1)
         scores = jnp.where(causal, scores * HD ** (-0.5), -jnp.inf)
         weights = jnp.exp(scores - jnp.max(scores, axis=-1, keepdims=True))
-        probs = (weights / jnp.sum(weights, axis=-1, keepdims=True)).astype(jnp.bfloat16)
-        ctx_in[n, y] = jnp.dot(probs, v, preferred_element_type=jnp.float32).astype(jnp.bfloat16)
+        mixed = jnp.dot(weights.astype(jnp.bfloat16), v, preferred_element_type=jnp.float32)
+        ctx_in[n, y] = (mixed / jnp.sum(weights, axis=-1, keepdims=True)).astype(jnp.bfloat16)
 
     def finish(n):
         with jax.named_scope("cwait1"):
@@ -238,42 +237,69 @@
         for k in (2, 1, 3):
             p_copy(n, 1, k, (y + k) % ny, s, at(0, k)).start()
         residual(n, res_src).wait_recv()
-        for i in (1, 0):
-            at_i = slice(i * (width // 2), (i + 1) * (width // 2))
-            total = res_in[n, :, at_i].astype(jnp.float32)
+
+        def total(i):
+            base = res_in[n, i].astype(jnp.float32)
             if i:
-                total = total + own_sum[y]
+                base = base + own_sum[y]
+            took = NEAR_FIRST + ((0,) if i == 0 else ())
             with jax.named_scope("pwait%d" % i):
-                for k in NEAR_FIRST + ((0,) if i == 0 else ()):
+                for k in took:
                     p_copy(n, i, k, 0, s, me).wait_recv()
-            for k in NEAR_FIRST + ((0,) if i == 0 else ()):
-                total = total + sums_in[n, i, k].astype(jnp.float32)
-            b_buf[n + 1, :, at_i] = total.astype(jnp.bfloat16)
-
-    def advance(n):
+            for k in took:
+                base = base + sums_in[n, i, k].astype(jnp.float32)
+            b_buf[n + 1, i] = base.astype(jnp.bfloat16)
+
+        def both(order):
+            for i in order:
+                total(i)
+
+                @pl.when(n < WAVES - 1)
+                def _():
+                    advance(n, i)
+
+                    @pl.when(gathers(s, n + 1))
+                    def _():
+                        x_send(n + 1, i, i == 0)
+
+            @pl.when(gathers(s, n + 1) & (n < WAVES - 1))
+            def _():
+                for i in order:
+                    x_send(n + 1, i, i == 1)
+
+        if ORDERED:
+            @pl.when(s % 2 == 0)
+            def _():
+                both((0, 1))
+
+            @pl.when(s % 2 == 1)
+            def _():
+                both((1, 0))
+        else:
+            both((1, 0))
+
+        @pl.when(runs(s, n + 1) & (n < WAVES - 1))
+        def _():
+            residual(n + 1, x_buf.at[n + 1, :, me]).start()
+
+    def advance(n, i):
         @pl.when(s == 0)
         def _():
-            settled = pick(sections - TICKS > lost, b_buf[TICKS], b_buf[TICKS + 1])
-            settled = pick(sections - 1 == lost, b_buf[1], settled)
-            x_buf[n + 1, me] = pick(n < TICKS, pool_ref[plan_ref[n]], settled)
+            settled = pick(sections - TICKS > lost, b_buf[TICKS, i], b_buf[TICKS + 1, i])
+            settled = pick(sections - 1 == lost, b_buf[1, i], settled)
+            x_buf[n + 1, i, me] = pick(n < TICKS, pool_ref[i, plan_ref[n]], settled)
 
         @pl.when(s != 0)
         def _():
-            x_buf[n + 1, me] = b_buf[n + 1]
-
-        @pl.when(gathers(s, n + 1))
-        def _():
-            x_send(n + 1)
-
-        @pl.when(runs(s, n + 1))
-        def _():
-            residual(n + 1, x_buf.at[n + 1, me]).start()
+            x_buf[n + 1, i, me] = b_buf[n + 1, i]
 
     def output():
         early = (s == 0) | (s < lost) | (s - TICKS > lost)
         for j in range(devices):
-            block = pick(early, x_buf[TICKS, j], x_buf[TICKS + 1, j])
-            later_hbm[0, :, j * width:(j + 1) * width] = pick(s == lost, jnp.zeros_like(block), block)
+            for i in range(2):
+                block = pick(early, x_buf[TICKS, i, j], x_buf[TICKS + 1, i, j])
+                at_i = slice(j * width + i * lanes, j * width + (i + 1) * lanes)
+                later_hbm[0, :, at_i] = pick(s == lost, jnp.zeros_like(block), block)
 
     pltpu.make_async_copy(wsrc_ref, wsrc_ref, local_sem.at[5]).wait()
     with jax.named_scope("bwait"):
@@ -282,7 +308,7 @@
     fold_half(1)
     colsum_ref[...] = jnp.broadcast_to(jnp.sum(colsum_ref[...], axis=0, keepdims=True), colsum_ref.shape)
     pltpu.make_async_copy(x_buf.at[0], x_buf.at[0], local_sem.at[1]).wait()
-    own = x_buf[0, me]
+    own = x_buf[0, :, me]
     res_src[...] = pick(s == lost, jnp.zeros_like(own), own)
     layer(0, True)
     c_send(0)
@@ -291,7 +317,7 @@
     with jax.named_scope("wwait"):
         took = wout_ref.at[0, pl.ds(0, cols)]
         pltpu.make_async_copy(took, took, local_sem.at[6]).wait()
-        took = x_buf.at[0, pl.ds(0, devices * (ny - 1) // 8)]
+        took = x_buf.at[0, 0, pl.ds(0, nz * (ny - 1))]
         pltpu.make_async_copy(took, took, wr.at[0]).wait()
         pltpu.make_async_copy(wout_ref.at[1], wout_ref.at[1], wr.at[1]).wait()
 
@@ -314,8 +340,8 @@
 
         @pl.when(gathers(s, n) & jnp.logical_not(runs(s, n)))
         def _():
-            for dz in (0,) + NEAR_FIRST:
-                x_settle(n, dz)
+            for blocks in GROUPS:
+                x_settle(n, blocks)
 
         @pl.when(n == WAVES - 1)
         def _():
@@ -329,12 +355,7 @@
 
         @pl.when(jnp.logical_not(runs(prv, n)))
         def _():
-            b_buf[n + 1] = jnp.zeros((rows, width), jnp.bfloat16)
-
-        @pl.when(n < WAVES - 1)
-        def _():
-            with jax.named_scope("advance"):
-                advance(n)
+            b_buf[n + 1] = jnp.zeros((2, rows, lanes), jnp.bfloat16)
 
         return carry
 
@@ -346,15 +367,17 @@
     wrapped = pick((last < lost) | (last - TICKS + 1 > lost), b_buf[TICKS + 1], b_buf[TICKS + 2])
     wrapped = pick(last == lost, b_buf[2], wrapped)
     settled = pick(s == 0, wrapped, settled)
-    standby_ref[0] = pick(s == 1, b_buf[TICKS + 2], settled)
-
-    sent = x_buf.at[0, pl.ds(0, devices * (2 * ny - 1) // 8)]
+    settled = pick(s == 1, b_buf[TICKS + 2], settled)
+    for i in range(2):
+        standby_ref[0, :, i * lanes:(i + 1) * lanes] = settled[i]
+
+    sent = x_buf.at[0:2, 0, pl.ds(0, nz * (2 * ny - 1) // 2)]
     pltpu.make_async_copy(sent, sent, ws).wait()
 
     def drain(n, carry):
         @pl.when(gathers(s, n))
         def _():
-            ref = x_buf.at[0, pl.ds(0, devices - 1)]
+            ref = x_buf.at[0, :, pl.ds(0, devices - 1)]
             pltpu.make_async_copy(ref, ref, xs.at[n]).wait()
 
         @pl.when(runs(s, n))
@@ -409,11 +432,11 @@
                 f32((8, 3 * cols)),
                 bf((cols, hidden)),
                 bf((2, ny * cols, nz * width // 2)),
-                bf((WAVES, devices, rows, width)),
-                bf((WAVES + 1, rows, width)),
-                bf(pool.shape),
-                bf((rows, width)),
-                bf((WAVES, rows, width)),
+                bf((WAVES, 2, devices, rows, width // 2)),
+                bf((WAVES + 1, 2, rows, width // 2)),
+                bf((2,) + pool.shape[:2] + (width // 2,)),
+                bf((2, rows, width // 2)),
+                bf((WAVES, 2, rows, width // 2)),
                 f32((rows, 3 * cols)),
                 f32((rows, width // 2)),
                 f32((rows, width // 2)),
@@ -421,7 +444,6 @@
                 bf((WAVES, nz + ny, rows, cols)),
                 bf((WAVES, 2, nz, rows, width // 2)),
                 bf((WAVES, 2, nz, rows, width // 2)),
-                bf((devices, rows, width)),
                 dma((8,)), dma, dma((2,)),
                 dma((WAVES,)), dma((WAVES, 2, devices)),
                 dma((WAVES,)), dma((WAVES, nz + ny)),

time: 103 us -> 101 us (0.981)
  Pallas kernels: 100 us -> 98.4 us
    pallas_call x1, Pallas kernels: 100 us -> 98.4 us  [per_device(): pl.pallas_call(functools.partial(relay_kernel, sections, nz, ny), out_sha...]
where the time goes in v5:
time: 101 us
  Pallas kernels  98.4 us (97%)
  local copies, waits for them, and re-layouts  1.6 us (2%)
  between operations  1.29 us (1%)
    pallas_call x1, Pallas kernels, per_device(): pl.pallas_call(functools.partial(relay_kernel, sections, nz, ny), out_sha...  98.4 us

profile of v5, /device:TPU:1, one launch (start us, length us, event | category | flops | bytes accessed | tf_op | source)
XLA Modules:
  0.0 101.2 jit_solution(10309535575000942105)
XLA Ops:
  1.3 98.4 %shard_map.86 = (bf16[1,128,4096]{2,1,0:T(8,128)(2,1)S(1)}, bf16[1,128,256]{2,1,0:T(8,128)(2,1)S(1)}) custom-call(s32[1]{0:T(128)S(6)} %copy.11.lost_ref, s32[4]{0:T(128)} %plan_ref.1, bf16[1,128,4096]{2,1,0:T(8,128)(2,1)} %pend_hbm.1, bf16[4,128,256]{2,1,0:T(8,128)(2,1)} %pool_hbm.1, bf16[3,4096,128]{2,1,0:T(8,128)(2,1)} %bitcast.4, ...), custom_call_target="tpu_custom_call" | custom-call | tf_op jit(solution)/shard_map/pallas_call | solution.py:421
  99.6 1.0 copy.12
  100.6 0.6 copy.13

commit v6 on v5

--- a/solution.py
+++ b/solution.py
@@ -25,9 +25,9 @@
 
 def relay_kernel(
     sections, nz, ny,
-    lost_ref, plan_ref, pend_hbm, pool_hbm, win_hbm, wout_hbm, gain_hbm,
+    lost_ref, plan_hbm, pend_hbm, pool_hbm, win_hbm, wout_hbm, gain_hbm,
     later_hbm, standby_ref,
-    win_ref, gain_ref, colsum_ref, wsrc_ref, wout_ref, x_buf, b_buf, pool_ref, res_src, res_in, acc, s1, s2, own_sum, ctx_in, sums_out, sums_in,
+    plan_ref, win_ref, gain_ref, colsum_ref, wsrc_ref, wout_ref, x_buf, b_buf, pool_ref, res_src, res_in, acc, s1, s2, own_sum, ctx_in, sums_out, sums_in,
     local_sem, ws, wr, xs, xr, cs, cr, ps, pr, rs, rr,
 ):
     s = lax.axis_index("section")
@@ -38,7 +38,6 @@
     rows, lanes = x_buf.shape[3], x_buf.shape[4]
     width = 2 * lanes
     cols = win_ref.shape[1] // 3
-    lost = lost_ref[0]
 
     def at(dz, dy):
         return ((z + dz) % nz) * ny + (y + dy) % ny
@@ -73,6 +72,7 @@
         pl.semaphore_signal(barrier, inc=1, device_id={"section": s, "tp": at(dz, dy)}, device_id_type=MESH)
 
     local(gain_hbm, gain_ref, 4).start()
+    local(plan_hbm, plan_ref, 9).start()
     depth = win_ref.shape[0] // 2
     for h in range(2):
         for i in range(3):
@@ -308,6 +308,8 @@
     fold_half(1)
     colsum_ref[...] = jnp.broadcast_to(jnp.sum(colsum_ref[...], axis=0, keepdims=True), colsum_ref.shape)
     pltpu.make_async_copy(x_buf.at[0], x_buf.at[0], local_sem.at[1]).wait()
+    local(plan_hbm, plan_ref, 9).wait()
+    lost = lost_ref[0]
     own = x_buf[0, :, me]
     res_src[...] = pick(s == lost, jnp.zeros_like(own), own)
     layer(0, True)
@@ -412,7 +414,6 @@
         cols = win.shape[3]
         win = jnp.transpose(win[0], (1, 0, 2))
         vmem = pl.BlockSpec(memory_space=pltpu.VMEM)
-        smem = pl.BlockSpec(memory_space=pltpu.SMEM)
         hbm = pl.BlockSpec(memory_space=pltpu.HBM)
         free = pl.BlockSpec(memory_space=pl.ANY)
         bf = functools.partial(pltpu.VMEM, dtype=jnp.bfloat16)
@@ -424,9 +425,10 @@
                 jax.ShapeDtypeStruct((1, rows, hidden), jnp.bfloat16),
                 jax.ShapeDtypeStruct((1, rows, width), jnp.bfloat16),
             ),
-            in_specs=[smem, smem, hbm, hbm, hbm, hbm, hbm],
+            in_specs=[pl.BlockSpec(memory_space=pltpu.SMEM)] + [hbm] * 6,
             out_specs=(vmem, vmem),
             scratch_shapes=[
+                pltpu.SMEM(plan.shape, jnp.int32),
                 bf((hidden, 3 * cols)),
                 bf(gain.shape),
                 f32((8, 3 * cols)),
@@ -444,7 +446,7 @@
                 bf((WAVES, nz + ny, rows, cols)),
                 bf((WAVES, 2, nz, rows, width // 2)),
                 bf((WAVES, 2, nz, rows, width // 2)),
-                dma((8,)), dma, dma((2,)),
+                dma((10,)), dma, dma((2,)),
                 dma((WAVES,)), dma((WAVES, 2, devices)),
                 dma((WAVES,)), dma((WAVES, nz + ny)),
                 dma((WAVES, 2)), dma((WAVES, 2, nz)),
@@ -453,7 +455,7 @@
             compiler_params=pltpu.CompilerParams(
                 collective_id=0, has_side_effects=True, vmem_limit_bytes=28 * 1024 * 1024
             ),
-        )(lost, *[pltpu.with_memory_space_constraint(a, pltpu.HBM) for a in (plan,)], *[pltpu.with_memory_space_constraint(a, pltpu.HBM) for a in (pend, pool, win, wout[0], gain)])
+        )(lost, *[pltpu.with_memory_space_constraint(a, pltpu.HBM) for a in (plan, pend, pool, win, wout[0], gain)])
 
     placed = (
         P("section", None, None),

time: 101 us -> 101 us (level)
  no operation moved by 1% of the time
where the time goes in v6:
time: 101 us
  Pallas kernels  97.7 us (97%)
  local copies, waits for them, and re-layouts  1.6 us (2%)
  between operations  1.29 us (1%)
    pallas_call x1, Pallas kernels, per_device(): pl.pallas_call(functools.partial(relay_kernel, sections, nz, ny), out_sha...  97.7 us

profile of v6, /device:TPU:1, one launch (start us, length us, event | category | flops | bytes accessed | tf_op | source)
XLA Modules:
  0.0 100.6 jit_solution(7919711332603708829)
XLA Ops:
  1.3 97.7 %shard_map.86 = (bf16[1,128,4096]{2,1,0:T(8,128)(2,1)S(1)}, bf16[1,128,256]{2,1,0:T(8,128)(2,1)S(1)}) custom-call(s32[1]{0:T(128)S(6)} %copy.11.lost_ref, s32[4]{0:T(128)} %plan_hbm.1, bf16[1,128,4096]{2,1,0:T(8,128)(2,1)} %pend_hbm.1, bf16[4,128,256]{2,1,0:T(8,128)(2,1)} %pool_hbm.1, bf16[3,4096,128]{2,1,0:T(8,128)(2,1)} %bitcast.4, ...), custom_call_target="tpu_custom_call" | custom-call | tf_op jit(solution)/shard_map/pallas_call | solution.py:422
  99.0 1.0 copy.12
  99.9 0.6 copy.13

commit v7 on v6

--- a/solution.py
+++ b/solution.py
@@ -135,10 +135,10 @@
     def x_forward(n):
         for k in NEAR_FIRST:
             x_copy(n, 0, at(k, 0), me).wait_recv()
-            for m in NEAR_FIRST:
+            for m in (NEAR_FIRST if k != 2 else (2, 1, 3)):
                 x_copy(n, 0, at(k, 0), at(0, m)).start()
             x_copy(n, 1, at(0, k), me).wait_recv()
-            for m in NEAR_FIRST:
+            for m in (NEAR_FIRST if k != 2 else (2, 1, 3)):
                 x_copy(n, 1, at(0, k), at(m, 0)).start()
 
     def x_settle(n, group):

time: 101 us -> 101 us (level)
  no operation moved by 1% of the time
where the time goes in v7:
time: 101 us; the launch traced here: 100 us
  Pallas kernels  97.6 us (97%)
  local copies, waits for them, and re-layouts  1.6 us (2%)
  between operations  1.29 us (1%)
    pallas_call x1, Pallas kernels, per_device(): pl.pallas_call(functools.partial(relay_kernel, sections, nz, ny), out_sha...  97.6 us

profile of v7, /device:TPU:1, one launch (start us, length us, event | category | flops | bytes accessed | tf_op | source)
XLA Modules:
  0.0 100.4 jit_solution(7491924977491647657)
XLA Ops:
  1.3 97.6 %shard_map.86 = (bf16[1,128,4096]{2,1,0:T(8,128)(2,1)S(1)}, bf16[1,128,256]{2,1,0:T(8,128)(2,1)S(1)}) custom-call(s32[1]{0:T(128)S(6)} %copy.11.lost_ref, s32[4]{0:T(128)} %plan_hbm.1, bf16[1,128,4096]{2,1,0:T(8,128)(2,1)} %pend_hbm.1, bf16[4,128,256]{2,1,0:T(8,128)(2,1)} %pool_hbm.1, bf16[3,4096,128]{2,1,0:T(8,128)(2,1)} %bitcast.4, ...), custom_call_target="tpu_custom_call" | custom-call | tf_op jit(solution)/shard_map/pallas_call | solution.py:422
  98.8 1.0 copy.12
  99.8 0.6 copy.13
